TPU v7x, 512 devices: a whole 4x8x8 slice. The times are simulated.
512 devices in a mesh: dp: 8 (over z_hi, core), mp: 64 (over z_lo, x, y).
Axes of the slice: x: 4, y: 8, z: 8 (z_hi: 4, z_lo: 2; z = z_hi * 2 + z_lo), core: 2. Of those that a mesh axis runs over, the one named last changes fastest.
Arguments:
- inputs: bfloat16 [2048, 4096], P('dp'), may hold values from -6 to 6
- upstream: bfloat16 [2048, 4096], P('dp'), may hold values from -6 to 6
- eig_tiles: bfloat16 [64, 8, 2, 128, 128], P('mp'), may hold values from -0.09375 to 0.09375
- eigvals: float32 [4096], replicated, may hold values from 0.25 to 4
Outputs:
- grad_t: bfloat16 [4096, 2048], P('mp', 'dp')
All inputs are finite; a program needn't handle non-finite values.
Results may differ from a plain program's by a relative error of at most 0.013.
Values may be sent and summed in bfloat16 or wider, within the bound.
No kernel may reach another device: no remote copies, remote signals or barrier semaphores. Data moves between devices by JAX's collectives and lax.ppermute only.
A program may use at most 64 MiB of HBM per device.

v0:
```python
import jax
import jax.numpy as jnp
from jax import lax
from jax.sharding import PartitionSpec as P


def split_up(value, dim, length):
    dims = value.shape
    blocks = value.reshape(*dims[:dim], length, dims[dim] // length, *dims[dim + 1 :])
    return jnp.moveaxis(blocks, dim, 0)


def summed_on_arrival(value, axis, dim):
    length = lax.axis_size(axis)
    blocks = lax.all_to_all(split_up(value, dim, length), axis, 0, 0, tiled=True)
    return jnp.sum(blocks.astype(jnp.float32), axis=0)


def laid_out(blocks, dim):
    blocks = jnp.moveaxis(blocks, 0, dim)
    dims = blocks.shape
    return blocks.reshape(*dims[:dim], dims[dim] * dims[dim + 1], *dims[dim + 2 :])


def copy_for_each(value, axis):
    length = lax.axis_size(axis)
    return lax.all_to_all(
        jnp.broadcast_to(value[None], (length, *value.shape)), axis, 0, 0, tiled=True
    )


def gather_directly(value, axis, dim):
    return laid_out(copy_for_each(value, axis), dim)


def kernel_of(left, right):
    root_left = jnp.sqrt(left)[:, None]
    root_right = jnp.sqrt(right)[None, :]
    return -1.0 / (root_left * root_right * (root_left + root_right))


def on_device(inputs, upstream, eig_tiles, eigvals):
    groups = lax.axis_size("mp")
    member = lax.axis_index("mp")
    width = eigvals.shape[0]
    slab = width // groups
    tile_rows = eig_tiles.shape[1]
    tile_cols = eig_tiles.shape[2]
    tile = eig_tiles.shape[3]
    grid_rows = width // (tile_rows * tile)
    grid_cols = groups // grid_rows
    piece = tile_cols * tile // groups
    local = jnp.transpose(eig_tiles[0], (0, 2, 1, 3)).reshape(tile_rows * tile, groups, piece)
    moved = lax.all_to_all(local, "mp", split_axis=1, concat_axis=1, tiled=True)
    moved = moved.reshape(tile_rows, tile, grid_rows, grid_cols, piece)
    basis = jnp.transpose(moved, (0, 2, 1, 3, 4)).reshape(width, slab)
    ordered = jnp.transpose(eigvals.reshape(tile_cols, grid_cols, tile), (1, 0, 2)).reshape(
        grid_cols, groups, piece
    )
    ordered = jnp.transpose(ordered, (1, 0, 2)).reshape(width)
    own = lax.dynamic_slice_in_dim(ordered, member * slab, slab)
    proj_in = jnp.dot(inputs, basis, preferred_element_type=jnp.float32).astype(jnp.bfloat16)
    proj_up = jnp.dot(upstream, basis, preferred_element_type=jnp.float32).astype(jnp.bfloat16)
    stacked = jnp.stack([proj_in, proj_up], 0)
    over_tokens = (((0,), (0,)), ((), ()))
    pieces = lax.all_gather(stacked, "mp", axis=2, tiled=True)
    part_in = pieces[0]
    part_up = pieces[1]
    block = lax.dot_general(proj_in, part_up, over_tokens, preferred_element_type=jnp.float32)
    block = block + lax.dot_general(
        proj_up, part_in, over_tokens, preferred_element_type=jnp.float32
    )
    joined = jnp.concatenate([block, part_in.astype(jnp.float32)], 0)
    gram = joined[:slab]
    all_in = joined[slab:].astype(jnp.bfloat16)
    share = summed_on_arrival(gram.astype(jnp.bfloat16), "dp", 0)
    count = share.shape[0]
    own_part = lax.dynamic_slice_in_dim(own, lax.axis_index("dp") * count, count)
    part = (kernel_of(own_part, ordered) * (0.5 * share)).astype(jnp.bfloat16)
    weighted = gather_directly(part, "dp", 0)
    over_columns = (((1,), (1,)), ((), ()))
    mixed = lax.dot_general(all_in, weighted, over_columns, preferred_element_type=jnp.float32)
    factor = 2.0 / (lax.axis_size("dp") * inputs.shape[0])
    update = (proj_up.astype(jnp.float32) / jnp.sqrt(own)[None, :] + factor * mixed).astype(
        jnp.bfloat16
    )
    own_rows = lax.all_to_all(basis, "mp", split_axis=0, concat_axis=1, tiled=True)
    every_update = gather_directly(update, "mp", 1)
    result = lax.dot_general(
        own_rows, every_update, over_columns, preferred_element_type=jnp.float32
    )
    return result.astype(jnp.bfloat16)


def solution(mesh):
    return jax.shard_map(
        on_device,
        mesh=mesh,
        in_specs=(P("dp", None), P("dp", None), P("mp", None, None, None, None), P()),
        out_specs=P("mp", "dp"),
        check_vma=False,
    )
```

profile of v0, /device:TPU:8, one launch (start us, length us, event | category | flops | bytes accessed | tf_op | source)
XLA Modules:
  0.0 494.4 jit_solution(2258323800576001424)
XLA Ops:
  6.5 0.0 copy-start
  6.5 0.0 all-gather.2.cloned.1.call-start
  6.5 1.5 copy.11
  8.0 0.1 reshape.93
  8.2 30.6 %all_to_all.36 = bf16[1024,64,4]{0,2,1:T(4,128)(2,1)S(1)} all-to-all(bf16[1024,64,4]{0,2,1:T(4,128)(2,1)S(1)} %reshape.93), channel_id=1, replica_groups=mesh['dp'=8,'mp'=64] {'mp'}, dimensions={1} | all-to-all | bytes 1048576 | tf_op jit(solution)/shard_map/all_to_all | solution.py:54
  38.7 1.0 reshape.102
  39.7 1.7 copy.13
  41.4 0.4 reshape.95
  41.8 0.0 copy-done
  41.8 0.0 copy-start.1
  41.8 0.8 convolution_convert_fusion.1
  42.6 0.8 copy-done.1
  43.4 0.8 convolution_convert_fusion
  44.2 0.6 pad_maximum_fusion
  44.8 0.0 all-gather.2.cloned.1.call-update
  44.8 303.2 %all-gather.2.cloned.1.call-done = bf16[2,256,4096]{1,2,0:T(8,128)(2,1)} async-done(((bf16[2,256,64]{1,2,0:T(8,128)(2,1)}), bf16[2,256,4096]{1,2,0:T(8,128)(2,1)}) %all-gather.2.cloned.1.call-update) | async-done | bytes 4194320 | tf_op jit(solution)/shard_map/all_gather | solution.py:66
  348.1 2.3 fusion.2
  350.4 0.0 copy-start.2
  350.4 3.2 fusion.1
  353.6 6.8 %all-to-all-start.1 = ((bf16[8,8,4096]{2,1,0:T(8,128)(2,1)}), bf16[8,8,4096]{2,1,0:T(8,128)(2,1)S(1)}, u32[]{:S(2)}, u32[]{:S(2)}) async-start(bf16[8,8,4096]{2,1,0:T(8,128)(2,1)} %fusion.1), calls=%async_computation.1 | async-start | bytes 1048576 | tf_op jit(solution)/shard_map/all_to_all | solution.py:15
  360.4 0.0 copy-done.2
  360.4 0.1 copy.14
  360.5 1.2 copy.15
  361.8 1.3 reshape.98
  363.1 0.1 dynamic-slice_sqrt_fusion
  363.2 15.2 %all-to-all-done.1 = bf16[8,8,4096]{2,1,0:T(8,128)(2,1)S(1)} async-done(((bf16[8,8,4096]{2,1,0:T(8,128)(2,1)}), bf16[8,8,4096]{2,1,0:T(8,128)(2,1)S(1)}, u32[]{:S(2)}, u32[]{:S(2)}) %all-to-all-start.1) | async-done | bytes 524320 | tf_op jit(solution)/shard_map/all_to_all | solution.py:15
  378.4 0.1 convert_reduce_fusion
  378.5 0.1 multiply_convert_fusion
  378.6 0.9 broadcast_in_dim.4
  379.4 3.5 all-to-all-start.2
  382.9 1.4 all_to_all.28
  384.3 2.9 copy.17
  387.3 3.0 reshape.103
  390.3 10.5 %all-to-all-done.2 = bf16[8,8,4096]{2,1,0:T(8,128)(2,1)S(1)} async-done(((bf16[8,8,4096]{2,1,0:T(8,128)(2,1)}), bf16[8,8,4096]{2,1,0:T(8,128)(2,1)S(1)}, u32[]{:S(2)}, u32[]{:S(2)}) %all-to-all-start.2) | async-done | bytes 524320 | tf_op jit(solution)/shard_map/all_to_all | solution.py:27
  400.8 8.2 %all-to-all-start.4 = ((bf16[64,2,2048]{2,1,0:T(2,128)(2,1)}), bf16[64,2,2048]{2,1,0:T(2,128)(2,1)S(1)}, u32[]{:S(2)}, u32[]{:S(2)}) async-start(bf16[64,2,2048]{2,1,0:T(2,128)(2,1)} %reshape.103), calls=%async_computation.4 | async-start | bytes 1048576 | tf_op jit(solution)/shard_map/all_to_all | solution.py:87
  409.0 0.1 dynamic-slice_sqrt_fusion.1
  409.1 2.1 fusion.11
  411.2 15.7 %all-to-all-done.4 = bf16[64,2,2048]{2,1,0:T(2,128)(2,1)S(1)} async-done(((bf16[64,2,2048]{2,1,0:T(2,128)(2,1)}), bf16[64,2,2048]{2,1,0:T(2,128)(2,1)S(1)}, u32[]{:S(2)}, u32[]{:S(2)}) %all-to-all-start.4) | async-done | bytes 524320 | tf_op jit(solution)/shard_map/all_to_all | solution.py:87
  426.9 1.6 broadcast_in_dim.5
  428.4 5.7 %all-to-all-start.3 = ((bf16[64,256,64]{1,2,0:T(8,128)(2,1)}), bf16[64,256,64]{1,2,0:T(8,128)(2,1)}, u32[]{:S(2)}, u32[]{:S(2)}) async-start(bf16[64,256,64]{1,2,0:T(8,128)(2,1)} %broadcast_in_dim.5), calls=%async_computation.3 | async-start | bytes 4194304 | tf_op jit(solution)/shard_map/all_to_all | solution.py:27
  434.2 1.6 reshape.104
  435.8 48.6 %all-to-all-done.3 = bf16[64,256,64]{1,2,0:T(8,128)(2,1)} async-done(((bf16[64,256,64]{1,2,0:T(8,128)(2,1)}), bf16[64,256,64]{1,2,0:T(8,128)(2,1)}, u32[]{:S(2)}, u32[]{:S(2)}) %all-to-all-start.3) | async-done | bytes 2097184 | tf_op jit(solution)/shard_map/all_to_all | solution.py:27
  484.5 3.0 fusion.15
  (1 shorter events, 0.0 us)
Async XLA Ops:
  6.5 35.3 %copy-start = (bf16[256,4096]{1,0:T(8,128)(2,1)S(1)}, bf16[256,4096]{1,0:T(8,128)(2,1)}, u32[]{:S(2)}) copy-start(bf16[256,4096]{1,0:T(8,128)(2,1)} %param.5) | copy-start | bytes 6291460
  6.5 341.5 %all-gather.2.cloned.1.call-start = ((), (), s32[]{:S(2)}) async-start(), calls=%async_computation.5 | async-start | bytes 4259840 | tf_op jit(solution)/shard_map/all_gather | solution.py:66
  41.8 1.6 copy-start.1
  350.4 10.0 %copy-start.2 = (f32[4096]{0:T(1024)S(1)}, f32[4096]{0:T(1024)}, u32[]{:S(2)}) copy-start(f32[4096]{0:T(1024)} %param.7) | copy-start | bytes 49156
  353.6 24.8 %all-to-all-start.1 = ((bf16[8,8,4096]{2,1,0:T(8,128)(2,1)}), bf16[8,8,4096]{2,1,0:T(8,128)(2,1)S(1)}, u32[]{:S(2)}, u32[]{:S(2)}) async-start(bf16[8,8,4096]{2,1,0:T(8,128)(2,1)} %fusion.1), calls=%async_computation.1 | async-start | bytes 1048576 | tf_op jit(solution)/shard_map/all_to_all | solution.py:15
  379.4 21.4 %all-to-all-start.2 = ((bf16[8,8,4096]{2,1,0:T(8,128)(2,1)}), bf16[8,8,4096]{2,1,0:T(8,128)(2,1)S(1)}, u32[]{:S(2)}, u32[]{:S(2)}) async-start(bf16[8,8,4096]{2,1,0:T(8,128)(2,1)} %broadcast_in_dim.4), calls=%async_computation.2 | async-start | bytes 1048576 | tf_op jit(solution)/shard_map/all_to_all | solution.py:27
  400.8 26.1 %all-to-all-start.4 = ((bf16[64,2,2048]{2,1,0:T(2,128)(2,1)}), bf16[64,2,2048]{2,1,0:T(2,128)(2,1)S(1)}, u32[]{:S(2)}, u32[]{:S(2)}) async-start(bf16[64,2,2048]{2,1,0:T(2,128)(2,1)} %reshape.103), calls=%async_computation.4 | async-start | bytes 1048576 | tf_op jit(solution)/shard_map/all_to_all | solution.py:87
  428.4 56.0 %all-to-all-start.3 = ((bf16[64,256,64]{1,2,0:T(8,128)(2,1)}), bf16[64,256,64]{1,2,0:T(8,128)(2,1)}, u32[]{:S(2)}, u32[]{:S(2)}) async-start(bf16[64,256,64]{1,2,0:T(8,128)(2,1)} %broadcast_in_dim.5), calls=%async_computation.3 | async-start | bytes 4194304 | tf_op jit(solution)/shard_map/all_to_all | solution.py:27
Sparse Core Ops, SparseCore 0:
  45.0 303.0 all-gather.1
where the time goes:
time: 495 us; the launch traced here: 494 us
  waiting for transfers between devices  393 us (79%)
  blocking collectives  30.6 us (6%)
  starting transfers between devices  24.3 us (5%)
  local copies, waits for them, and re-layouts  19.8 us (4%)
  between operations  13.5 us (3%)
  matrix products  12.1 us (2%)
    all_gather x1, waiting for transfers between devices, on_device(): pieces = lax.all_gather(stacked, 'mp', axis=2, tiled=True)  303 us
    all_to_all x2, waiting for transfers between devices, copy_for_each(): lax.all_to_all(jnp.broadcast_to(value[None], (length, *value.shape)), axi...  59.2 us
    all_to_all x1, blocking collectives, on_device(): moved = lax.all_to_all(local, 'mp', split_axis=1, concat_axis=1, tiled=True)  30.6 us
    all_to_all x1, waiting for transfers between devices, on_device(): lax.all_to_all(basis, 'mp', split_axis=0, concat_axis=1, tiled=True)  15.7 us
    all_to_all x1, waiting for transfers between devices, summed_on_arrival(): lax.all_to_all(split_up(value, dim, length), axis, 0, 0, tiled=True)  15.2 us
  transfers between devices with their start and end apart: 5, of which 5 were waited for; matrix products, arithmetic and copies ran while one was open for 3% of the time, Pallas kernels for 0%

commit v1 on v0

--- a/solution.py
+++ b/solution.py
@@ -63,7 +63,7 @@
     proj_up = jnp.dot(upstream, basis, preferred_element_type=jnp.float32).astype(jnp.bfloat16)
     stacked = jnp.stack([proj_in, proj_up], 0)
     over_tokens = (((0,), (0,)), ((), ()))
-    pieces = lax.all_gather(stacked, "mp", axis=2, tiled=True)
+    pieces = jnp.concatenate(lax.all_gather(stacked, "mp"), axis=2)
     part_in = pieces[0]
     part_up = pieces[1]
     block = lax.dot_general(proj_in, part_up, over_tokens, preferred_element_type=jnp.float32)

time: 495 us -> 496 us (level)
  transfers between devices with their start and end apart: 5 -> 5, of which waited for: 5 -> 5; matrix products, arithmetic and copies ran while one was open for 3% -> 2% of each run, Pallas kernels for 0% -> 0%
where the time goes in v1:
time: 496 us; the launch traced here: 495 us
  waiting for transfers between devices  395 us (80%)
  blocking collectives  30.6 us (6%)
  starting transfers between devices  24.8 us (5%)
  local copies, waits for them, and re-layouts  21.5 us (4%)
  between operations  13.5 us (3%)
  matrix products  8.75 us (2%)
    all_gather x1, waiting for transfers between devices, on_device(): pieces = jnp.concatenate(lax.all_gather(stacked, 'mp'), axis=2)  303 us
    all_to_all x2, waiting for transfers between devices, copy_for_each(): lax.all_to_all(jnp.broadcast_to(value[None], (length, *value.shape)), axi...  60.7 us
    all_to_all x1, blocking collectives, on_device(): moved = lax.all_to_all(local, 'mp', split_axis=1, concat_axis=1, tiled=True)  30.6 us
    all_to_all x1, waiting for transfers between devices, on_device(): lax.all_to_all(basis, 'mp', split_axis=0, concat_axis=1, tiled=True)  16 us
    all_to_all x1, waiting for transfers between devices, summed_on_arrival(): lax.all_to_all(split_up(value, dim, length), axis, 0, 0, tiled=True)  15.5 us
  transfers between devices with their start and end apart: 5, of which 5 were waited for; matrix products, arithmetic and copies ran while one was open for 2% of the time, Pallas kernels for 0%

profile of v1, /device:TPU:8, one launch (start us, length us, event | category | flops | bytes accessed | tf_op | source)
XLA Modules:
  0.0 495.2 jit_solution(15396127786331049673)
XLA Ops:
  6.5 0.0 copy-start
  6.5 0.0 all-gather.3.cloned.1.call-start
  6.5 1.5 copy.18
  8.0 0.1 reshape.101
  8.2 30.6 %all_to_all.36 = bf16[1024,64,4]{0,2,1:T(4,128)(2,1)S(1)} all-to-all(bf16[1024,64,4]{0,2,1:T(4,128)(2,1)S(1)} %reshape.101), channel_id=1, replica_groups=mesh['dp'=8,'mp'=64] {'mp'}, dimensions={1} | all-to-all | bytes 1048576 | tf_op jit(solution)/shard_map/all_to_all | solution.py:54
  38.7 1.0 reshape.112
  39.7 1.7 copy.20
  41.4 0.4 reshape.103
  41.8 0.0 copy-done
  41.8 0.0 copy-start.3
  41.8 0.8 convolution_convert_fusion.1
  42.6 0.8 copy-done.3
  43.4 0.8 convolution_convert_fusion
  44.2 0.6 pad_maximum_fusion
  44.8 0.0 all-gather.3.cloned.1.call-update
  44.8 303.0 %all-gather.3.cloned.1.call-done = bf16[128,256,64]{1,2,0:T(8,128)(2,1)} async-done(((bf16[2,256,64]{1,2,0:T(8,128)(2,1)}), bf16[128,256,64]{1,2,0:T(8,128)(2,1)}) %all-gather.3.cloned.1.call-update) | async-done | bytes 4194320 | tf_op jit(solution)/shard_map/all_gather | solution.py:66
  347.9 2.7 fusion.17
  350.6 0.0 copy-start.1
  350.6 0.7 fusion.18
  351.4 0.6 copy-done.1
  352.0 0.0 copy-start.4
  352.0 1.6 fusion.1
  353.5 6.8 %all-to-all-start.1 = ((bf16[8,8,4096]{2,1,0:T(8,128)(2,1)}), bf16[8,8,4096]{2,1,0:T(8,128)(2,1)S(1)}, u32[]{:S(2)}, u32[]{:S(2)}) async-start(bf16[8,8,4096]{2,1,0:T(8,128)(2,1)} %fusion.1), calls=%async_computation.1 | async-start | bytes 1048576 | tf_op jit(solution)/shard_map/all_to_all | solution.py:15
  360.3 0.0 copy-done.4
  360.3 0.1 copy.21
  360.4 1.2 copy.22
  361.7 1.3 reshape.106
  363.0 0.1 dynamic-slice_sqrt_fusion
  363.1 15.5 %all-to-all-done.1 = bf16[8,8,4096]{2,1,0:T(8,128)(2,1)S(1)} async-done(((bf16[8,8,4096]{2,1,0:T(8,128)(2,1)}), bf16[8,8,4096]{2,1,0:T(8,128)(2,1)S(1)}, u32[]{:S(2)}, u32[]{:S(2)}) %all-to-all-start.1) | async-done | bytes 524320 | tf_op jit(solution)/shard_map/all_to_all | solution.py:15
  378.6 0.1 convert_reduce_fusion
  378.6 0.1 multiply_convert_fusion
  378.7 0.8 broadcast_in_dim.4
  379.6 4.1 all-to-all-start.2
  383.7 1.4 all_to_all.28
  385.1 2.2 copy.24
  387.3 1.5 reshape.113
  388.9 12.6 %all-to-all-done.2 = bf16[8,8,4096]{2,1,0:T(8,128)(2,1)} async-done(((bf16[8,8,4096]{2,1,0:T(8,128)(2,1)}), bf16[8,8,4096]{2,1,0:T(8,128)(2,1)}, u32[]{:S(2)}, u32[]{:S(2)}) %all-to-all-start.2) | async-done | bytes 524320 | tf_op jit(solution)/shard_map/all_to_all | solution.py:27
  401.5 8.1 %all-to-all-start.4 = ((bf16[64,2,2048]{2,1,0:T(2,128)(2,1)}), bf16[64,2,2048]{2,1,0:T(2,128)(2,1)S(1)}, u32[]{:S(2)}, u32[]{:S(2)}) async-start(bf16[64,2,2048]{2,1,0:T(2,128)(2,1)} %reshape.113), calls=%async_computation.4 | async-start | bytes 1048576 | tf_op jit(solution)/shard_map/all_to_all | solution.py:87
  409.6 0.1 dynamic-slice_sqrt_fusion.1
  409.7 2.2 fusion.8
  411.9 16.0 %all-to-all-done.4 = bf16[64,2,2048]{2,1,0:T(2,128)(2,1)S(1)} async-done(((bf16[64,2,2048]{2,1,0:T(2,128)(2,1)}), bf16[64,2,2048]{2,1,0:T(2,128)(2,1)S(1)}, u32[]{:S(2)}, u32[]{:S(2)}) %all-to-all-start.4) | async-done | bytes 524320 | tf_op jit(solution)/shard_map/all_to_all | solution.py:87
  427.9 0.0 copy-start.2
  427.9 1.6 broadcast_in_dim.5
  429.4 0.0 copy-done.2
  429.5 5.8 %all-to-all-start.3 = ((bf16[64,256,64]{1,2,0:T(8,128)(2,1)}), bf16[64,256,64]{1,2,0:T(8,128)(2,1)}, u32[]{:S(2)}, u32[]{:S(2)}) async-start(bf16[64,256,64]{1,2,0:T(8,128)(2,1)} %broadcast_in_dim.5), calls=%async_computation.3 | async-start | bytes 4194304 | tf_op jit(solution)/shard_map/all_to_all | solution.py:27
  435.2 2.3 reshape.114
  437.5 48.1 %all-to-all-done.3 = bf16[64,256,64]{1,2,0:T(8,128)(2,1)} async-done(((bf16[64,256,64]{1,2,0:T(8,128)(2,1)}), bf16[64,256,64]{1,2,0:T(8,128)(2,1)}, u32[]{:S(2)}, u32[]{:S(2)}) %all-to-all-start.3) | async-done | bytes 2097184 | tf_op jit(solution)/shard_map/all_to_all | solution.py:27
  485.6 2.7 fusion.12
  (1 shorter events, 0.0 us)
Async XLA Ops:
  6.5 35.3 %copy-start = (bf16[256,4096]{1,0:T(8,128)(2,1)S(1)}, bf16[256,4096]{1,0:T(8,128)(2,1)}, u32[]{:S(2)}) copy-start(bf16[256,4096]{1,0:T(8,128)(2,1)} %param.5) | copy-start | bytes 6291460
  6.5 341.3 %all-gather.3.cloned.1.call-start = ((), (), s32[]{:S(2)}) async-start(), calls=%async_computation.5 | async-start | bytes 4259840 | tf_op jit(solution)/shard_map/all_gather | solution.py:66
  41.8 1.6 copy-start.3
  350.6 1.3 copy-start.1
  352.0 8.3 %copy-start.4 = (f32[4096]{0:T(1024)S(1)}, f32[4096]{0:T(1024)}, u32[]{:S(2)}) copy-start(f32[4096]{0:T(1024)} %param.7) | copy-start | bytes 49156
  353.5 25.0 %all-to-all-start.1 = ((bf16[8,8,4096]{2,1,0:T(8,128)(2,1)}), bf16[8,8,4096]{2,1,0:T(8,128)(2,1)S(1)}, u32[]{:S(2)}, u32[]{:S(2)}) async-start(bf16[8,8,4096]{2,1,0:T(8,128)(2,1)} %fusion.1), calls=%async_computation.1 | async-start | bytes 1048576 | tf_op jit(solution)/shard_map/all_to_all | solution.py:15
  379.6 21.9 %all-to-all-start.2 = ((bf16[8,8,4096]{2,1,0:T(8,128)(2,1)}), bf16[8,8,4096]{2,1,0:T(8,128)(2,1)}, u32[]{:S(2)}, u32[]{:S(2)}) async-start(bf16[8,8,4096]{2,1,0:T(8,128)(2,1)} %broadcast_in_dim.4), calls=%async_computation.2 | async-start | bytes 1048576 | tf_op jit(solution)/shard_map/all_to_all | solution.py:27
  401.5 26.4 %all-to-all-start.4 = ((bf16[64,2,2048]{2,1,0:T(2,128)(2,1)}), bf16[64,2,2048]{2,1,0:T(2,128)(2,1)S(1)}, u32[]{:S(2)}, u32[]{:S(2)}) async-start(bf16[64,2,2048]{2,1,0:T(2,128)(2,1)} %reshape.113), calls=%async_computation.4 | async-start | bytes 1048576 | tf_op jit(solution)/shard_map/all_to_all | solution.py:87
  427.9 1.6 copy-start.2
  429.5 56.2 %all-to-all-start.3 = ((bf16[64,256,64]{1,2,0:T(8,128)(2,1)}), bf16[64,256,64]{1,2,0:T(8,128)(2,1)}, u32[]{:S(2)}, u32[]{:S(2)}) async-start(bf16[64,256,64]{1,2,0:T(8,128)(2,1)} %broadcast_in_dim.5), calls=%async_computation.3 | async-start | bytes 4194304 | tf_op jit(solution)/shard_map/all_to_all | solution.py:27
Sparse Core Ops, SparseCore 0:
  45.0 302.8 all-gather.2
